TPU v7x, 32 devices: a whole 2x2x4 slice. The times are simulated.
32 devices in a mesh: texel: 8 (over y, x, core), light: 4 (over z).
Axes of the slice: x: 2, y: 2, z: 4, core: 2. Of those that a mesh axis runs over, the one named last changes fastest.
Arguments:
- tex_feat: bfloat16 [8192, 512], P('texel'), may hold values from -18 to 18
- light_feat: bfloat16 [6144, 512], P('light'), may hold values from -0.25 to 0.25
- sketch: bfloat16 [6144, 256], P('light'), may hold values from -0.078125 to 0.078125
- row_counts: int32 [8], replicated, may hold values from 1 to 1024, 4096 in all
Outputs:
- basis: float32 [8192, 256], P('texel')
- coeffs: float32 [256, 6144], P('texel', 'light')
Inputs may be any that keep to these rules, and one draw needn't show every extreme that they name: row_counts sums to 8 * 512; some entry equals 1024.
All inputs are finite; a program needn't handle non-finite values.
Results may differ from a plain program's by a relative error of at most 0.0034.
Values sent between devices are 32-bit elements; how exact they have to be, the bound alone decides.
A program may use at most 64 MiB of HBM per device.

v0:
```python
import jax
import jax.numpy as jnp
from jax import lax
from jax.sharding import PartitionSpec as P


def on_device(tex_feat, light_feat, sketch, row_counts):
    capacity = tex_feat.shape[0]
    own_count = row_counts[lax.axis_index("texel")]
    valid_total = jnp.sum(row_counts).astype(jnp.float32)
    logits = lax.dot_general(
        tex_feat, light_feat, (((1,), (1,)), ((), ())), preferred_element_type=jnp.float32
    )
    tile_block = jnp.sin(logits).astype(jnp.bfloat16)
    row_valid = (lax.iota(jnp.int32, capacity) < own_count).astype(jnp.float32)
    partial_value = (
        jnp.dot(tile_block, sketch, preferred_element_type=jnp.float32) * row_valid[:, None]
    )
    sketched = lax.psum(partial_value, "light")
    gram_local = jnp.dot(sketched.T, sketched, precision=lax.Precision.HIGHEST)
    gram_matrix = lax.psum(gram_local, "texel") / valid_total
    factor = jnp.linalg.cholesky(gram_matrix)
    basis = jax.scipy.linalg.solve_triangular(factor, sketched.T, lower=True).T
    basis_half = basis.astype(jnp.bfloat16)
    coeffs = lax.psum_scatter(
        lax.dot_general(
            basis_half, tile_block, (((0,), (0,)), ((), ())), preferred_element_type=jnp.float32
        ),
        "texel",
        scatter_dimension=0,
        tiled=True,
    ) / jnp.sqrt(valid_total)
    return (basis, coeffs)


def solution(mesh):
    placed = (P("texel", None), P("light", None), P("light", None), P())
    return jax.shard_map(
        on_device,
        mesh=mesh,
        in_specs=placed,
        out_specs=(P("texel", None), P("texel", "light")),
        check_vma=False,
    )
```

profile of v0, /device:TPU:0, one launch (start us, length us, event | category | flops | bytes accessed | tf_op | source)
XLA Modules:
  0.0 261.9 jit_solution(2642677506085759507)
XLA Ops:
  7.2 0.0 copy-start
  7.2 0.0 all-reduce.4.cloned.1.call-start
  7.2 1.3 dynamic_slice.3
  8.6 0.6 fusion.10
  9.2 0.0 copy-done
  9.2 0.0 copy-start.4
  9.3 23.0 %sine_convert_fusion = bf16[1024,1536]{1,0:T(8,128)(2,1)S(1)} fusion(bf16[1024,512]{1,0:T(8,128)(2,1)} %param.4, bf16[1536,512]{1,0:T(8,128)(2,1)S(1)} %copy-done), kind=kOutput, calls=%fused_computation.2 | convolution fusion | flops 1612185600 | bytes 5767168 | tf_op jit(solution)/shard_map/dot_general | solution.py:11
  32.2 0.0 copy-start.2
  32.2 1.7 copy-done.2
  33.9 0.0 copy-done.4
  33.9 1.9 convolution_multiply_fusion
  35.8 0.0 copy-start.6
  35.8 0.0 all-reduce.4.cloned.1.call-update
  35.9 0.0 all-reduce.6.cloned.1.call-start
  35.9 54.7 %all-reduce.4.cloned.1.call-done = f32[1024,256]{1,0:T(8,128)} async-done(((f32[1024,256]{1,0:T(8,128)}), f32[1024,256]{1,0:T(8,128)}) %all-reduce.4.cloned.1.call-update) | async-done | bytes 1048592 | tf_op jit(solution)/shard_map/psum | solution.py:19
  90.6 0.0 copy-start.1
  90.6 4.1 %fusion.12 = f32[256,256]{0,1:T(8,128)} fusion(f32[1024,256]{1,0:T(8,128)} %all-reduce.4.cloned.1.call-done), kind=kOutput, calls=%fused_computation.37 | convolution fusion | flops 805306368 | bytes 1310720 | tf_op jit(solution)/shard_map/dot_general | solution.py:20
  94.8 0.0 all-reduce.6.cloned.1.call-update
  94.8 0.2 reduce-scatter.2.cloned.1.call-start
  95.0 0.0 copy-done.6
  95.1 0.6 reduce_sum.9
  96.3 51.8 %all-reduce.6.cloned.1.call-done = f32[256,256]{0,1:T(8,128)} async-done(((f32[256,256]{0,1:T(8,128)}), f32[256,256]{0,1:T(8,128)}) %all-reduce.6.cloned.1.call-update) | async-done | bytes 262160 | tf_op jit(solution)/shard_map/psum | solution.py:21
  148.1 1.0 broadcast_divide_fusion
  149.1 0.1 copy.7
  149.2 1.0 fusion.4
  150.2 11.7 %cholesky.50 = f32[128,128]{1,0:T(8,128)S(1)} custom-call(f32[128,128]{1,0:T(8,128)S(1)} %cholesky.118), custom_call_target="Cholesky" | custom-call | tf_op jit(solution)/shard_map/jit(cholesky)/cholesky | solution.py:22
  162.0 9.8 %custom-call.15 = f32[1,128,128]{1,2,0:T(8,128)S(1)} custom-call(f32[1,128,128]{2,1,0:T(8,128)S(1)} %get-tuple-element.25), custom_call_target="InvertDiagBlocksLowerTriangular" | custom-call | tf_op jit(solution)/shard_map/jit(cholesky)/cholesky | solution.py:22
  171.8 0.2 constant_dynamic-update-slice_fusion.1
  172.0 0.3 convolution_subtract_fusion.1
  172.3 11.7 %cholesky.105 = f32[128,128]{1,0:T(8,128)S(1)} custom-call(f32[128,128]{1,0:T(8,128)S(1)} %convolution_subtract_fusion.1), custom_call_target="Cholesky" | custom-call | tf_op jit(solution)/shard_map/jit(cholesky)/cholesky | solution.py:22
  184.1 0.7 compare_reduce_fusion
  186.0 0.1 triangular_solve.57
  186.1 4.1 %while.1 = (s32[]{:T(128)}, f32[256,256]{1,0:T(8,128)S(1)}, s32[2,2]{1,0:T(2,128)S(1)}, f32[2,128,128]{2,1,0:T(8,128)S(1)}, s32[]{:T(128)}) while((s32[]{:T(128)}, f32[256,256]{1,0:T(8,128)S(1)}, s32[2,2]{1,0:T(2,128)S(1)}, f32[2,128,128]{2,1,0:T(8,128)S(1)}, s32[]{:T(128)}) %tuple.28), condition=%wide.while_cond, body=%wide.while_body.sunk | while | flops 2 | bytes 131189 | solution.py:23
  186.3 0.6 fusion.25
  186.9 1.4 bitcast_dynamic-update-slice_fusion.2
  188.3 0.6 fusion.25
  188.8 1.4 bitcast_dynamic-update-slice_fusion.2
  190.2 0.0 copy-start.5
  190.2 0.6 copy-done.5
  190.9 20.5 %custom-call.16 = f32[2,128,128]{1,2,0:T(8,128)S(1)} custom-call(f32[2,128,128]{2,1,0:T(8,128)} %copy-done.5), custom_call_target="InvertDiagBlocksLowerTriangular" | custom-call | tf_op jit(solution)/shard_map/jit(_solve_triangular)/triangular_solve | solution.py:23
  211.4 0.0 copy-start.3
  211.4 0.0 copy-done.1
  211.4 0.6 fusion
  212.0 1.0 convolution_subtract_fusion
  213.0 0.6 fusion.6
  213.7 0.0 copy-done.3
  213.7 2.2 fusion.2
  215.9 0.0 reduce-scatter.2.cloned.1.call-update
  215.9 1.1 maximum_bitcast_fusion
  217.0 2.5 copy.8
  219.5 34.2 %reduce-scatter.2.cloned.1.call-done = f32[32,1536]{1,0:T(8,128)} async-done(((f32[256,1536]{1,0:T(8,128)}), f32[32,1536]{1,0:T(8,128)}) %reduce-scatter.2.cloned.1.call-update) | async-done | bytes 196624 | tf_op jit(solution)/shard_map/reduce_scatter | solution.py:25
  253.7 1.6 broadcast_divide_fusion.1
  (9 shorter events, 0.1 us)
Async XLA Ops:
  7.2 2.1 copy-start
  7.2 83.5 %all-reduce.4.cloned.1.call-start = ((), (), s32[]{:S(2)}) async-start(), calls=%async_computation.1 | async-start | bytes 2097152 | tf_op jit(solution)/shard_map/psum | solution.py:19
  9.2 24.7 %copy-start.4 = (bf16[1536,256]{1,0:T(8,128)(2,1)S(1)}, bf16[1536,256]{1,0:T(8,128)(2,1)}, u32[]{:S(2)}) copy-start(bf16[1536,256]{1,0:T(8,128)(2,1)} %param.6) | copy-start | bytes 2359300
  32.2 1.7 copy-start.2
  35.8 59.2 %copy-start.6 = (s32[8]{0:T(128)S(1)}, s32[8]{0:T(128)}, u32[]{:S(2)}) copy-start(s32[8]{0:T(128)} %param.7) | copy-start | bytes 100
  35.9 112.3 %all-reduce.6.cloned.1.call-start = ((), (), s32[]{:S(2)}) async-start(), calls=%async_computation.2 | async-start | bytes 524288 | tf_op jit(solution)/shard_map/psum | solution.py:21
  90.6 120.7 %copy-start.1 = (f32[1024,256]{1,0:T(8,128)S(1)}, f32[1024,256]{1,0:T(8,128)}, u32[]{:S(2)}) copy-start(f32[1024,256]{1,0:T(8,128)} %all-reduce.4.cloned.1.call-done) | copy-start | bytes 3145732
  94.8 158.9 %reduce-scatter.2.cloned.1.call-start = ((), (), s32[]{:S(2)}) async-start(), calls=%async_computation.3 | async-start | bytes 1769472 | tf_op jit(solution)/shard_map/reduce_scatter | solution.py:25
  190.2 0.7 copy-start.5
  211.4 2.3 copy-start.3
Sparse Core Ops, SparseCore 0:
  36.0 54.6 all-reduce.3
  94.9 53.1 all-reduce.5
  216.0 37.6 reduce-scatter.1
where the time goes:
time: 262 us
  waiting for transfers between devices  141 us (54%)
  other arithmetic  60.4 us (23%)
  matrix products  34 us (13%)
  between operations  15.8 us (6%)
  local copies, waits for them, and re-layouts  10.3 us (4%)
    psum x1, waiting for transfers between devices, on_device(): sketched = lax.psum(partial_value, 'light')  54.7 us
    psum x1, waiting for transfers between devices, on_device(): gram_matrix = lax.psum(gram_local, 'texel') / valid_total  51.8 us
    reduce_scatter x1, waiting for transfers between devices, on_device(): lax.psum_scatter(lax.dot_general(basis_half, tile_block, (((0,), (0,)), (...  34.2 us
    another operation x6, other arithmetic, on_device(): factor = jnp.linalg.cholesky(gram_matrix)  34 us
    dot_general x1, matrix products, on_device(): lax.dot_general(tex_feat, light_feat, (((1,), (1,)), ((), ())), preferred...  23 us
    another operation x3, other arithmetic, on_device(): basis = jax.scipy.linalg.solve_triangular(factor, sketched.T, lower=True).T  20.5 us
  transfers between devices with their start and end apart: 3, of which 3 were waited for; matrix products, arithmetic and copies ran while one was open for 2% of the time, Pallas kernels for 0%

commit v1 on v0

--- a/solution.py
+++ b/solution.py
@@ -16,7 +16,12 @@
     partial_value = (
         jnp.dot(tile_block, sketch, preferred_element_type=jnp.float32) * row_valid[:, None]
     )
-    sketched = lax.psum(partial_value, "light")
+    slots = lax.axis_size("light")
+    sketched, f_next = (partial_value, 0)
+    while 1 << f_next < slots:
+        spare = lax.ppermute(sketched, "light", [(i, i ^ 1 << f_next) for i in range(slots)])
+        sketched = sketched + spare
+        f_next = f_next + 1
     gram_local = jnp.dot(sketched.T, sketched, precision=lax.Precision.HIGHEST)
     gram_matrix = lax.psum(gram_local, "texel") / valid_total
     factor = jnp.linalg.cholesky(gram_matrix)

time: 262 us -> 283 us (1.080)
  waiting for transfers between devices: 141 us -> 154 us
  starting transfers between devices: 0.3 us -> 6.18 us
    ppermute x0 -> x2, waiting for transfers between devices: none -> 66.8 us  [on_device(): lax.ppermute(sketched, 'light', [(i, i ^ 1 << f_next) for i in range(slot...]
    psum x1 -> x0, waiting for transfers between devices: 54.7 us -> none  [on_device(): sketched = lax.psum(partial_value, 'light')]
    ppermute x0 -> x2, starting transfers between devices: none -> 5.92 us  [on_device(): lax.ppermute(sketched, 'light', [(i, i ^ 1 << f_next) for i in range(slot...]
  transfers between devices with their start and end apart: 3 -> 4, of which waited for: 3 -> 4; matrix products, arithmetic and copies ran while one was open for 2% -> 2% of each run, Pallas kernels for 0% -> 0%
where the time goes in v1:
time: 283 us
  waiting for transfers between devices  154 us (54%)
  other arithmetic  62.9 us (22%)
  matrix products  34 us (12%)
  between operations  16.3 us (6%)
  local copies, waits for them, and re-layouts  9.45 us (3%)
  starting transfers between devices  6.18 us (2%)
    ppermute x2, waiting for transfers between devices, on_device(): lax.ppermute(sketched, 'light', [(i, i ^ 1 << f_next) for i in range(slot...  66.8 us
    psum x1, waiting for transfers between devices, on_device(): gram_matrix = lax.psum(gram_local, 'texel') / valid_total  52.5 us
    reduce_scatter x1, waiting for transfers between devices, on_device(): lax.psum_scatter(lax.dot_general(basis_half, tile_block, (((0,), (0,)), (...  34.2 us
    another operation x6, other arithmetic, on_device(): factor = jnp.linalg.cholesky(gram_matrix)  34 us
    dot_general x1, matrix products, on_device(): lax.dot_general(tex_feat, light_feat, (((1,), (1,)), ((), ())), preferred...  23 us
    another operation x3, other arithmetic, on_device(): basis = jax.scipy.linalg.solve_triangular(factor, sketched.T, lower=True).T  20.5 us
    ppermute x2, starting transfers between devices, on_device(): lax.ppermute(sketched, 'light', [(i, i ^ 1 << f_next) for i in range(slot...  5.92 us
  transfers between devices with their start and end apart: 4, of which 4 were waited for; matrix products, arithmetic and copies ran while one was open for 2% of the time, Pallas kernels for 0%

profile of v1, /device:TPU:0, one launch (start us, length us, event | category | flops | bytes accessed | tf_op | source)
XLA Modules:
  0.0 282.6 jit_solution(2622502421054951745)
XLA Ops:
  7.2 0.0 copy-start
  7.2 0.0 all-reduce.3.cloned.1.call-start
  7.2 1.3 dynamic_slice.3
  8.6 0.6 fusion.13
  9.2 0.0 copy-done
  9.2 0.0 copy-start.4
  9.3 23.0 %sine_convert_fusion = bf16[1024,1536]{1,0:T(8,128)(2,1)S(1)} fusion(bf16[1024,512]{1,0:T(8,128)(2,1)} %param.4, bf16[1536,512]{1,0:T(8,128)(2,1)S(1)} %copy-done), kind=kOutput, calls=%fused_computation.2 | convolution fusion | flops 1612185600 | bytes 5767168 | tf_op jit(solution)/shard_map/dot_general | solution.py:11
  32.2 0.0 copy-done.4
  32.2 0.0 copy-start.2
  32.2 1.0 convolution_multiply_fusion
  33.2 0.7 copy-done.2
  33.9 0.0 copy-start.6
  33.9 3.1 %collective-permute-start = (f32[1024,256]{1,0:T(8,128)S(1)}, f32[1024,256]{1,0:T(8,128)S(1)}, u32[]{:S(2)}, u32[]{:S(2)}) collective-permute-start(f32[1024,256]{1,0:T(8,128)S(1)} %convolution_multiply_fusion), channel_id=1, source_target_pairs={{0,1},{1,0},{2,3},{3,2},{4,5},{5,4},{6,7},{7,6},{8,9},{9,8},{10,11... | collective-permute-start | bytes 3145736 | tf_op jit(solution)/shard_map/ppermute | solution.py:22
  37.0 23.1 %collective-permute-done = f32[1024,256]{1,0:T(8,128)S(1)} collective-permute-done((f32[1024,256]{1,0:T(8,128)S(1)}, f32[1024,256]{1,0:T(8,128)S(1)}, u32[]{:S(2)}, u32[]{:S(2)}) %collective-permute-start) | collective-permute-done | bytes 1048608 | tf_op jit(solution)/shard_map/ppermute | solution.py:22
  60.1 0.1 add.37
  60.2 2.8 %collective-permute-start.1 = (f32[1024,256]{1,0:T(8,128)S(1)}, f32[1024,256]{1,0:T(8,128)}, u32[]{:S(2)}, u32[]{:S(2)}) collective-permute-start(f32[1024,256]{1,0:T(8,128)S(1)} %add.37), channel_id=1, source_target_pairs={{0,2},{1,3},{2,0},{3,1},{4,6},{5,7},{6,4},{7,5},{8,10},{9,11},{10,... | collective-permute-start | bytes 3145736 | tf_op jit(solution)/shard_map/ppermute | solution.py:22
  63.1 0.0 copy-done.6
  63.1 0.6 reduce_sum.9
  64.4 43.7 %collective-permute-done.1 = f32[1024,256]{1,0:T(8,128)} collective-permute-done((f32[1024,256]{1,0:T(8,128)S(1)}, f32[1024,256]{1,0:T(8,128)}, u32[]{:S(2)}, u32[]{:S(2)}) %collective-permute-start.1) | collective-permute-done | bytes 1048608 | tf_op jit(solution)/shard_map/ppermute | solution.py:22
  108.1 4.1 %fusion.5 = f32[256,256]{0,1:T(8,128)} fusion(f32[1024,256]{1,0:T(8,128)S(1)} %add.37, f32[1024,256]{1,0:T(8,128)} %collective-permute-done.1), kind=kOutput, calls=%fused_computation.13 | convolution fusion | flops 805568512 | bytes 2359296 | tf_op jit(solution)/shard_map/dot_general | solution.py:25
  112.2 0.0 all-reduce.3.cloned.1.call-update
  112.2 0.2 reduce-scatter.2.cloned.1.call-start
  112.4 2.3 add_bitcast_fusion
  114.7 0.0 copy-start.1
  114.7 52.5 %all-reduce.3.cloned.1.call-done = f32[256,256]{0,1:T(8,128)} async-done(((f32[256,256]{0,1:T(8,128)}), f32[256,256]{0,1:T(8,128)}) %all-reduce.3.cloned.1.call-update) | async-done | bytes 262160 | tf_op jit(solution)/shard_map/psum | solution.py:26
  167.2 1.0 broadcast_divide_fusion
  168.2 0.1 copy.7
  168.3 1.0 fusion.7
  169.4 11.7 %cholesky.50 = f32[128,128]{1,0:T(8,128)S(1)} custom-call(f32[128,128]{1,0:T(8,128)S(1)} %cholesky.118), custom_call_target="Cholesky" | custom-call | tf_op jit(solution)/shard_map/jit(cholesky)/cholesky | solution.py:27
  181.1 9.8 %custom-call.15 = f32[1,128,128]{1,2,0:T(8,128)S(1)} custom-call(f32[1,128,128]{2,1,0:T(8,128)S(1)} %get-tuple-element.25), custom_call_target="InvertDiagBlocksLowerTriangular" | custom-call | tf_op jit(solution)/shard_map/jit(cholesky)/cholesky | solution.py:27
  190.9 0.2 constant_dynamic-update-slice_fusion.1
  191.2 0.3 convolution_subtract_fusion
  191.4 11.7 %cholesky.105 = f32[128,128]{1,0:T(8,128)S(1)} custom-call(f32[128,128]{1,0:T(8,128)S(1)} %convolution_subtract_fusion), custom_call_target="Cholesky" | custom-call | tf_op jit(solution)/shard_map/jit(cholesky)/cholesky | solution.py:27
  203.2 0.7 compare_reduce_fusion
  205.3 0.1 triangular_solve.57
  205.3 4.2 %while.1 = (s32[]{:T(128)}, f32[256,256]{1,0:T(8,128)S(1)}, s32[2,2]{1,0:T(2,128)S(1)}, f32[2,128,128]{2,1,0:T(8,128)S(1)}, s32[]{:T(128)}) while((s32[]{:T(128)}, f32[256,256]{1,0:T(8,128)S(1)}, s32[2,2]{1,0:T(2,128)S(1)}, f32[2,128,128]{2,1,0:T(8,128)S(1)}, s32[]{:T(128)}) %tuple.28), condition=%wide.while_cond, body=%wide.while_body.sunk | while | flops 2 | bytes 131189 | solution.py:28
  205.5 0.6 fusion.24
  206.1 1.4 bitcast_dynamic-update-slice_fusion.2
  207.5 0.6 fusion.24
  208.1 1.4 bitcast_dynamic-update-slice_fusion.2
  209.6 0.0 copy-start.5
  209.6 0.6 copy-done.5
  210.2 20.5 %custom-call.16 = f32[2,128,128]{1,2,0:T(8,128)S(1)} custom-call(f32[2,128,128]{2,1,0:T(8,128)} %copy-done.5), custom_call_target="InvertDiagBlocksLowerTriangular" | custom-call | tf_op jit(solution)/shard_map/jit(_solve_triangular)/triangular_solve | solution.py:28
  230.7 0.0 copy-done.1
  230.7 0.0 copy-start.3
  230.7 0.6 fusion.1
  231.4 1.0 fusion.8
  232.4 1.7 fusion
  234.1 0.0 copy-done.3
  234.1 2.2 fusion.3
  236.2 0.0 reduce-scatter.2.cloned.1.call-update
  236.3 1.0 maximum_bitcast_fusion
  237.4 2.5 copy.8
  239.9 34.2 %reduce-scatter.2.cloned.1.call-done = f32[32,1536]{1,0:T(8,128)} async-done(((f32[256,1536]{1,0:T(8,128)}), f32[32,1536]{1,0:T(8,128)}) %reduce-scatter.2.cloned.1.call-update) | async-done | bytes 196624 | tf_op jit(solution)/shard_map/reduce_scatter | solution.py:30
  274.1 1.6 broadcast_divide_fusion.1
  (9 shorter events, 0.1 us)
Async XLA Ops:
  7.2 2.1 copy-start
  7.2 160.1 %all-reduce.3.cloned.1.call-start = ((), (), s32[]{:S(2)}) async-start(), calls=%async_computation.1 | async-start | bytes 524288 | tf_op jit(solution)/shard_map/psum | solution.py:26
  9.2 23.0 %copy-start.4 = (bf16[1536,256]{1,0:T(8,128)(2,1)S(1)}, bf16[1536,256]{1,0:T(8,128)(2,1)}, u32[]{:S(2)}) copy-start(bf16[1536,256]{1,0:T(8,128)(2,1)} %param.6) | copy-start | bytes 2359300
  32.2 1.7 copy-start.2
  33.9 29.2 %copy-start.6 = (s32[8]{0:T(128)S(1)}, s32[8]{0:T(128)}, u32[]{:S(2)}) copy-start(s32[8]{0:T(128)} %param.7) | copy-start | bytes 100
  33.9 26.2 %collective-permute-start = (f32[1024,256]{1,0:T(8,128)S(1)}, f32[1024,256]{1,0:T(8,128)S(1)}, u32[]{:S(2)}, u32[]{:S(2)}) collective-permute-start(f32[1024,256]{1,0:T(8,128)S(1)} %convolution_multiply_fusion), channel_id=1, source_target_pairs={{0,1},{1,0},{2,3},{3,2},{4,5},{5,4},{6,7},{7,6},{8,9},{9,8},{10,11... | collective-permute-start | bytes 3145736 | tf_op jit(solution)/shard_map/ppermute | solution.py:22
  60.2 47.8 %collective-permute-start.1 = (f32[1024,256]{1,0:T(8,128)S(1)}, f32[1024,256]{1,0:T(8,128)}, u32[]{:S(2)}, u32[]{:S(2)}) collective-permute-start(f32[1024,256]{1,0:T(8,128)S(1)} %add.37), channel_id=1, source_target_pairs={{0,2},{1,3},{2,0},{3,1},{4,6},{5,7},{6,4},{7,5},{8,10},{9,11},{10,... | collective-permute-start | bytes 3145736 | tf_op jit(solution)/shard_map/ppermute | solution.py:22
  112.2 161.9 %reduce-scatter.2.cloned.1.call-start = ((), (), s32[]{:S(2)}) async-start(), calls=%async_computation.2 | async-start | bytes 1769472 | tf_op jit(solution)/shard_map/reduce_scatter | solution.py:30
  114.7 116.0 %copy-start.1 = (f32[256,1024]{0,1:T(8,128)S(1)}, f32[256,1024]{0,1:T(8,128)}, u32[]{:S(2)}) copy-start(f32[256,1024]{0,1:T(8,128)} %add_bitcast_fusion) | copy-start | bytes 3145732
  209.6 0.7 copy-start.5
  230.7 3.3 %copy-start.3 = (bf16[1024,1536]{1,0:T(8,128)(2,1)S(1)}, bf16[1024,1536]{1,0:T(8,128)(2,1)}, u32[]{:S(2)}) copy-start(bf16[1024,1536]{1,0:T(8,128)(2,1)} %copy-done.2) | copy-start | bytes 9437188
Sparse Core Ops, SparseCore 0:
  112.3 54.8 all-reduce.2
  236.4 37.6 reduce-scatter.1
